TPU v7x, 32 devices: a whole 2x2x4 slice. The times are simulated.
32 devices in a mesh: rep: 32 (over z, y, x, core).
Axes of the slice: x: 2, y: 2, z: 4, core: 2. Of those that a mesh axis runs over, the one named last changes fastest.
Arguments:
- inputs: bfloat16 [16384, 1024], P('rep'), may hold values from -6 to 6
- out_grads: bfloat16 [16384, 4096], P('rep'), may hold values from -0.29882812 to 0.29882812
- error_in: bfloat16 [32, 1024, 4096], P('rep'), may hold values from -6 to 6
- q_start: float32 [32, 4096], replicated, may hold values from -0.09375 to 0.09375
- master: float32 [1024, 4096], P(None, 'rep'), may hold values from -1.2 to 1.2
Outputs:
- error_out: bfloat16 [32, 1024, 4096], P('rep')
- q_out: float32 [32, 4096], replicated
- master_out: float32 [1024, 4096], P(None, 'rep')
All inputs are finite; a program needn't handle non-finite values.
Results may differ from a plain program's by a relative error of at most 0.001.
Values sent between devices are 32-bit elements; how exact they have to be, the bound alone decides.
A program may use at most 128 MiB of HBM per device.

v0:
```python
import jax
import jax.numpy as jnp
from jax import lax
from jax.sharding import PartitionSpec as P

ITERS = 3


def orthonormal(rows):
    basis = jnp.zeros_like(rows)
    for k in range(rows.shape[0]):
        vector = rows[k]
        coef = jnp.dot(basis, vector, precision=lax.Precision.HIGHEST)
        vector = vector - jnp.dot(coef, basis, precision=lax.Precision.HIGHEST)
        basis = basis.at[k].set(vector / jnp.sqrt(jnp.sum(vector * vector) + 1.0))
    return basis


def outer_rows(left, right):
    return lax.dot_general(
        left,
        right,
        (((0,), (0,)), ((), ())),
        precision=lax.Precision.HIGHEST,
        preferred_element_type=jnp.float32,
    )


def shards(inputs, out_grads, error_in, q_start, master):
    count = lax.axis_size("rep")
    grad = lax.dot_general(
        inputs, out_grads, (((0,), (0,)), ((), ())), preferred_element_type=jnp.float32
    )
    merged = grad + error_in[0].astype(jnp.float32)
    factor = q_start
    basis = None
    local_q = None
    for step in range(ITERS):
        local_p = lax.dot_general(
            factor,
            merged,
            (((1,), (1,)), ((), ())),
            precision=lax.Precision.HIGHEST,
            preferred_element_type=jnp.float32,
        )
        total_p = lax.psum(local_p, "rep")
        basis = orthonormal(total_p)
        local_q = jnp.dot(
            basis, merged, precision=lax.Precision.HIGHEST, preferred_element_type=jnp.float32
        )
        if step + 1 < ITERS:
            factor = lax.psum(local_q, "rep") / count
    width = master.shape[1]
    factor = lax.psum(local_q, "rep") / count
    recon = outer_rows(basis, factor)
    own_cols = lax.dynamic_slice_in_dim(recon, lax.axis_index("rep") * width, width, 1)
    master_out = master - 0.5 * own_cols
    error_out = (merged - recon).astype(jnp.bfloat16)[None]
    return (error_out, factor, master_out)


def solution(mesh):
    return jax.shard_map(
        shards,
        mesh=mesh,
        in_specs=(P("rep", None), P("rep", None), P("rep", None, None), P(), P(None, "rep")),
        out_specs=(P("rep", None, None), P(), P(None, "rep")),
        check_vma=False,
    )
```

profile of v0, /device:TPU:27, one launch (start us, length us, event | category | flops | bytes accessed | tf_op | source)
XLA Modules:
  0.0 1162.8 jit_solution(7776026956208568537)
XLA Ops:
  7.2 1.2 copy-done
  8.4 8.8 convert_add_fusion
  17.2 5.7 copy-done.1
  22.9 16.0 %convolution_bitcast_fusion = f32[32,1024]{1,0:T(8,128)} fusion(f32[1024,4096]{1,0:T(8,128)S(1)} %convert_add_fusion, f32[32,4096]{1,0:T(8,128)S(1)} %copy-done.3), kind=kOutput, calls=%fused_computation.3 | convolution fusion | flops 1610612736 | bytes 17432576 | tf_op jit(solution)/shard_map/dot_general | solution.py:39
  39.1 122.7 %all-reduce.10.cloned.1.call-done = f32[32,1024]{1,0:T(8,128)} async-done(((f32[32,1024]{1,0:T(8,128)}), f32[32,1024]{1,0:T(8,128)}) %all-reduce.10.cloned.1.call-update) | async-done | bytes 131088 | tf_op jit(solution)/shard_map/psum | solution.py:46
  162.9 1.2 fusion.236
  168.0 0.9 convolution_bitcast_fusion.94
  173.2 0.9 convolution_bitcast_fusion.92
  175.7 0.9 convolution_bitcast_fusion.91
  178.3 0.9 convolution_bitcast_fusion.90
  186.1 0.9 convolution_bitcast_fusion.87
  188.7 0.9 convolution_bitcast_fusion.86
  193.9 0.9 convolution_bitcast_fusion.84
  196.5 0.9 convolution_bitcast_fusion.83
  197.6 1.3 fusion.235
  200.4 0.9 convolution_bitcast_fusion.82
  203.0 0.9 convolution_bitcast_fusion.81
  208.1 0.9 convolution_bitcast_fusion.79
  210.7 0.9 convolution_bitcast_fusion.78
  213.3 0.9 convolution_bitcast_fusion.77
  215.9 0.9 convolution_bitcast_fusion.76
  218.5 0.9 convolution_bitcast_fusion.75
  223.7 0.9 convolution_bitcast_fusion.73
  228.8 0.9 convolution_bitcast_fusion.71
  234.0 0.9 convolution_bitcast_fusion.69
  236.6 0.9 convolution_bitcast_fusion.68
  239.2 0.9 convolution_bitcast_fusion.67
  241.8 0.9 convolution_bitcast_fusion.66
  244.4 0.9 convolution_bitcast_fusion.65
  247.2 13.9 %fusion.267 = f32[32,4096]{1,0:T(8,128)} fusion(f32[32,1024]{1,0:T(8,128)S(1)} %scatter.371, f32[1024,4096]{1,0:T(8,128)} %copy-done.1), kind=kOutput, calls=%fused_computation.560 | convolution fusion | flops 1610612736 | bytes 17432576 | tf_op jit(solution)/shard_map/dot_general | solution.py:48
  261.1 128.2 %all-reduce.12.cloned.1.call-done = f32[32,4096]{1,0:T(8,128)} async-done(((f32[32,4096]{1,0:T(8,128)}), f32[32,4096]{1,0:T(8,128)}) %all-reduce.12.cloned.1.call-update) | async-done | bytes 524304 | tf_op jit(solution)/shard_map/psum | solution.py:52
  389.4 19.3 %fusion.3 = f32[32,1024]{1,0:T(8,128)} fusion(f32[1024,4096]{1,0:T(8,128)} %copy-done.1, f32[32,4096]{1,0:T(8,128)} %all-reduce.12.cloned.1.call-done), kind=kOutput, calls=%fused_computation.103 | convolution fusion | flops 1610743808 | bytes 17432576 | tf_op jit(solution)/shard_map/dot_general | solution.py:39
  408.7 123.6 %all-reduce.14.cloned.1.call-done = f32[32,1024]{1,0:T(8,128)} async-done(((f32[32,1024]{1,0:T(8,128)}), f32[32,1024]{1,0:T(8,128)}) %all-reduce.14.cloned.1.call-update) | async-done | bytes 131088 | tf_op jit(solution)/shard_map/psum | solution.py:46
  533.4 1.2 fusion.234
  538.5 0.9 convolution_bitcast_fusion.62
  541.1 0.9 convolution_bitcast_fusion.61
  568.6 1.3 fusion.233
  617.9 13.9 %fusion.298 = f32[32,4096]{1,0:T(8,128)} fusion(f32[32,1024]{1,0:T(8,128)S(1)} %scatter.425, f32[1024,4096]{1,0:T(8,128)} %copy-done.1), kind=kOutput, calls=%fused_computation.591 | convolution fusion | flops 1610612736 | bytes 17432576 | tf_op jit(solution)/shard_map/dot_general | solution.py:48
  632.1 128.1 %all-reduce.16.cloned.1.call-done = f32[32,4096]{1,0:T(8,128)} async-done(((f32[32,4096]{1,0:T(8,128)}), f32[32,4096]{1,0:T(8,128)}) %all-reduce.16.cloned.1.call-update) | async-done | bytes 524304 | tf_op jit(solution)/shard_map/psum | solution.py:52
  760.1 19.3 %fusion.1 = f32[32,1024]{1,0:T(8,128)} fusion(f32[1024,4096]{1,0:T(8,128)} %copy-done.1, f32[32,4096]{1,0:T(8,128)} %all-reduce.16.cloned.1.call-done), kind=kOutput, calls=%fused_computation.101 | convolution fusion | flops 1610743808 | bytes 17432576 | tf_op jit(solution)/shard_map/dot_general | solution.py:39
  779.5 123.6 %all-reduce.18.cloned.1.call-done = f32[32,1024]{1,0:T(8,128)} async-done(((f32[32,1024]{1,0:T(8,128)}), f32[32,1024]{1,0:T(8,128)}) %all-reduce.18.cloned.1.call-update) | async-done | bytes 131088 | tf_op jit(solution)/shard_map/psum | solution.py:46
  904.2 1.2 fusion.232
  938.9 1.3 fusion.231
  988.2 14.1 %fusion.329 = f32[32,4096]{1,0:T(8,128)} fusion(f32[32,1024]{1,0:T(8,128)S(1)} %scatter.479, f32[1024,4096]{1,0:T(8,128)} %copy-done.1), kind=kOutput, calls=%fused_computation.622 | convolution fusion | flops 1610612736 | bytes 17432576 | tf_op jit(solution)/shard_map/dot_general | solution.py:48
  1002.3 128.2 %all-reduce.20.cloned.1.call-done = f32[32,4096]{1,0:T(8,128)} async-done(((f32[32,4096]{1,0:T(8,128)}), f32[32,4096]{1,0:T(8,128)}) %all-reduce.20.cloned.1.call-update) | async-done | bytes 524304 | tf_op jit(solution)/shard_map/psum | solution.py:54
  1130.6 1.1 broadcast_multiply_fusion
  1131.7 13.6 %fusion.330 = f32[1024,4096]{1,0:T(8,128)S(1)} fusion(f32[32,1024]{1,0:T(8,128)S(1)} %scatter.479, f32[32,4096]{1,0:T(8,128)S(1)} %broadcast_multiply_fusion), kind=kOutput, calls=%fused_computation.623 | convolution fusion | flops 1610612736 | bytes 17432576 | tf_op jit(solution)/shard_map/dot_general | solution.py:20
  1145.3 9.6 fusion
  (477 shorter events, 158.8 us)
Async XLA Ops:
  7.2 1.2 copy-start
  7.2 15.7 %copy-start.3 = (f32[32,4096]{1,0:T(8,128)S(1)}, f32[32,4096]{1,0:T(8,128)}, u32[]{:S(2)}) copy-start(f32[32,4096]{1,0:T(8,128)} %param.200) | copy-start | bytes 1572868
  7.2 154.7 %all-reduce.10.cloned.1.call-start = ((), (), s32[]{:S(2)}) async-start(), calls=%async_computation | async-start | bytes 262144 | tf_op jit(solution)/shard_map/psum | solution.py:46
  17.2 5.7 copy-start.1
  38.9 350.5 %all-reduce.12.cloned.1.call-start = ((), (), s32[]{:S(2)}) async-start(), calls=%async_computation.1 | async-start | bytes 1048576 | tf_op jit(solution)/shard_map/psum | solution.py:52
  261.1 271.2 %all-reduce.14.cloned.1.call-start = ((), (), s32[]{:S(2)}) async-start(), calls=%async_computation.2 | async-start | bytes 262144 | tf_op jit(solution)/shard_map/psum | solution.py:46
  408.7 351.5 %all-reduce.16.cloned.1.call-start = ((), (), s32[]{:S(2)}) async-start(), calls=%async_computation.3 | async-start | bytes 1048576 | tf_op jit(solution)/shard_map/psum | solution.py:52
  631.9 271.2 %all-reduce.18.cloned.1.call-start = ((), (), s32[]{:S(2)}) async-start(), calls=%async_computation.4 | async-start | bytes 262144 | tf_op jit(solution)/shard_map/psum | solution.py:46
  779.4 351.1 %all-reduce.20.cloned.1.call-start = ((), (), s32[]{:S(2)}) async-start(), calls=%async_computation.5 | async-start | bytes 1048576 | tf_op jit(solution)/shard_map/psum | solution.py:54
  1131.7 23.2 %copy-start.2 = (f32[32,4096]{1,0:T(8,128)}, f32[32,4096]{1,0:T(8,128)S(1)}, u32[]{:S(2)}) copy-start(f32[32,4096]{1,0:T(8,128)S(1)} %broadcast_multiply_fusion) | copy-start | bytes 1572868
  1145.3 9.6 copy-start.4
Sparse Core Ops, SparseCore 0:
  39.0 122.7 all-reduce.9
  261.2 128.0 all-reduce.11
  408.8 123.5 all-reduce.13
  632.0 128.1 all-reduce.15
  779.6 123.4 all-reduce.17
  1002.5 128.0 all-reduce.19
where the time goes:
time: 1180 us; the launch traced here: 1160 us
  waiting for transfers between devices  755 us (64%)
  matrix products  229 us (19%)
  between operations  83.2 us (7%)
  other arithmetic  69.8 us (6%)
  local copies, waits for them, and re-layouts  25.2 us (2%)
    psum x3, waiting for transfers between devices, shards(): factor = lax.psum(local_q, 'rep') / count  384 us
    psum x3, waiting for transfers between devices, shards(): total_p = lax.psum(local_p, 'rep')  370 us
    dot_general x96, matrix products, orthonormal(): coef = jnp.dot(basis, vector, precision=lax.Precision.HIGHEST)  89.7 us
    reduce_sum x96, other arithmetic, orthonormal(): basis = basis.at[k].set(vector / jnp.sqrt(jnp.sum(vector * vector) + 1.0))  57.8 us
    dot_general x3, matrix products, shards(): lax.dot_general(factor, merged, (((1,), (1,)), ((), ())), precision=lax.P...  54.5 us
    dot_general x3, matrix products, shards(): jnp.dot(basis, merged, precision=lax.Precision.HIGHEST, preferred_element...  41.9 us
  transfers between devices with their start and end apart: 6, of which 6 were waited for; matrix products, arithmetic and copies ran while one was open for 0% of the time, Pallas kernels for 0%

commit v1 on v0

v1 whole, which is shorter than its diff:
```python
import functools

import jax
import jax.numpy as jnp
from jax import lax
from jax.experimental import pallas as pl
from jax.experimental.pallas import tpu as pltpu
from jax.sharding import PartitionSpec as P

ITERS = 3
AXIS = "rep"
MESH = pl.DeviceIdType.MESH
F32, BF16 = jnp.float32, jnp.bfloat16


def split_tiles(count, rows, cols):
    col_cuts = min(count, cols // 128)
    row_cuts = max(1, min(count // col_cuts, rows // 8))
    return row_cuts, col_cuts, count // (row_cuts * col_cuts)


def halves(value):
    high = value.astype(BF16)
    return high, (value - high.astype(F32)).astype(BF16)


def kernel(
    count, x_hbm, dy_hbm, err_hbm, start_ref, master_ref,
    err_out, q_out, master_out,
    x_v, xt_v, dy_v, m_hi, m_lo,
    q_full, q_part, q_recv, q_split, p_full, p_part, p_recv, vecs, basis, b_split, b_tall, p_tall,
    load_sem, dy_sem, err_sem,
    p_rs_send, p_rs_recv, p_ag_send, p_ag_recv, q_rs_send, q_rs_recv, q_ag_send, q_ag_recv,
):
    me = lax.axis_index(AXIS)
    err_v = err_out.at[0]
    rank, width = p_full.shape
    ff = q_full.shape[1]
    step_cols = dy_sem.shape[0]
    cw = ff // step_cols

    pltpu.make_async_copy(x_hbm, x_v, load_sem).start()
    for c in range(step_cols):
        cols = pl.ds(c * cw, cw)
        pltpu.make_async_copy(dy_hbm.at[:, cols], dy_v.at[:, cols], dy_sem.at[c]).start()
        pltpu.make_async_copy(err_hbm.at[0, :, cols], err_v.at[:, cols], err_sem.at[c]).start()

    barrier = pltpu.get_barrier_semaphore()

    @pl.loop(1, count)
    def _(d):
        pl.semaphore_signal(barrier, inc=1, device_id=(lax.rem(me + d, count),), device_id_type=MESH)

    def piece(cuts, shape, owner):
        row_cuts, col_cuts, stride = cuts
        index = owner // stride
        rows, cols = shape[0] // row_cuts, shape[1] // col_cuts
        row = pl.multiple_of((index % row_cuts) * rows, rows)
        col = pl.multiple_of((index // row_cuts) * cols, cols)
        return pl.ds(row, rows), pl.ds(col, cols)

    def is_owner(cuts, device):
        return lax.rem(device, cuts[2]) == 0

    def guarded(cuts, device, body):
        if cuts[2] == 1:
            body()
        else:
            pl.when(is_owner(cuts, device))(body)

    def send_piece(cuts, part, recv, send_sem, recv_sem, target):
        def body():
            pltpu.make_async_remote_copy(
                src_ref=part.at[piece(cuts, part.shape, target)],
                dst_ref=recv.at[lax.rem(target - me + count, count) - 1],
                send_sem=send_sem, recv_sem=recv_sem,
                device_id=(target,), device_id_type=MESH,
            ).start()
        guarded(cuts, target, body)

    def drain(recv, sem, pieces):
        if pieces:
            ref = recv.at[pl.ds(0, pieces)]
            pltpu.make_async_copy(ref, ref, sem).wait()

    def either(cuts, owner_body, other_body):
        if cuts[2] == 1:
            owner_body()
        else:
            pl.when(is_owner(cuts, me))(owner_body)
            pl.when(jnp.logical_not(is_owner(cuts, me)))(other_body)

    def add_up(cuts, part, full, recv, recv_sem, ag_send, ag_recv, scale):
        def body():
            mine = piece(cuts, part.shape, me)
            drain(recv, recv_sem, count - 1)
            total = part[mine] + jnp.sum(recv[...], axis=0)
            full[mine] = total if scale == 1 else total / scale

            @pl.loop(1, count)
            def _(d):
                pltpu.make_async_remote_copy(
                    src_ref=full.at[mine], dst_ref=full.at[mine],
                    send_sem=ag_send, recv_sem=ag_recv,
                    device_id=(lax.rem(me + d, count),), device_id_type=MESH,
                ).start()

        either(cuts, body, lambda: None)

    def drain_sends(cuts, recv, rs_send, ag_send):
        owners = cuts[0] * cuts[1]

        def owner_body():
            drain(recv, rs_send, owners - 1)
            drain(recv, ag_send, count - 1)

        either(cuts, owner_body, lambda: drain(recv, rs_send, owners))

    p_cuts = split_tiles(count, rank, width)
    q_cuts = split_tiles(count, rank, ff)
    q_width = ff // q_cuts[1]
    members = cw // q_width * q_cuts[0]
    own_group = me // q_cuts[2] // members

    def columns(group):
        return pl.ds(pl.multiple_of(group * cw, cw), cw)

    def await_group(group):
        either(
            q_cuts,
            lambda: own_or_other(group),
            lambda: drain(q_recv, q_ag_recv.at[group], members),
        )

    def own_or_other(group):
        @pl.when(group == own_group)
        def _():
            drain(q_recv, q_ag_recv.at[group], members - 1)

        @pl.when(group != own_group)
        def _():
            drain(q_recv, q_ag_recv.at[group], members)

    def absorb(source, cols):
        high, low = halves(source[:, cols])
        factor = jnp.concatenate([high, low], axis=0)
        dims = (((1,), (1,)), ((), ()))
        tall = lax.dot_general(m_hi[:, cols], factor, dims, preferred_element_type=F32)
        tall += lax.dot_general(m_lo[:, cols], factor, dims, preferred_element_type=F32)
        p_tall[...] += tall

    def settle():
        flat = p_tall[...].T
        p_part[...] = flat[0:rank] + flat[rank:2 * rank]
        p_tall[...] = jnp.zeros_like(p_tall)

    pltpu.make_async_copy(x_hbm, x_v, load_sem).wait()
    xt_v[...] = x_v[...].T
    p_tall[...] = jnp.zeros_like(p_tall)

    @pl.loop(0, step_cols)
    def _(c):
        cols = pl.ds(pl.multiple_of(c * cw, cw), cw)
        pltpu.make_async_copy(dy_hbm.at[:, cols], dy_v.at[:, cols], dy_sem.at[c]).wait()
        pltpu.make_async_copy(err_hbm.at[0, :, cols], err_v.at[:, cols], err_sem.at[c]).wait()
        merged = jnp.dot(xt_v[...], dy_v[:, cols], preferred_element_type=F32)
        high, low = halves(merged + err_v[:, cols].astype(F32))
        m_hi[:, cols] = high
        m_lo[:, cols] = low
        absorb(start_ref, cols)

    settle()
    pl.semaphore_wait(barrier, count - 1)

    @pl.loop(0, ITERS)
    def _(step):
        @pl.loop(1, count)
        def _(d):
            send_piece(p_cuts, p_part, p_recv, p_rs_send, p_rs_recv, lax.rem(me + d, count))

        add_up(p_cuts, p_part, p_full, p_recv, p_rs_recv, p_ag_send, p_ag_recv, 1)
        p_owners = p_cuts[0] * p_cuts[1]
        either(
            p_cuts,
            lambda: drain(p_recv, p_ag_recv, p_owners - 1),
            lambda: drain(p_recv, p_ag_recv, p_owners),
        )
        drain_sends(p_cuts, p_recv, p_rs_send, p_ag_send)

        vecs[...] = p_full[...]
        for base in range(0, rank, 8):
            block = pl.ds(base, 8)
            above, rest = p_full[block, :], vecs[block, :]
            done = []
            for k in range(8):
                row = rest[k:k + 1, :]
                norm = jnp.sum(row * row, axis=1, keepdims=True) + 1.0
                coef = jnp.sum(above * row, axis=1, keepdims=True)
                inverse = lax.rsqrt(norm)
                unit = row * inverse
                done.append(unit)
                if k < 7:
                    rest = rest - (coef * inverse) * unit
                for below in range(base + 8, rank, 8):
                    later = pl.ds(below, 8)
                    coef = jnp.sum(p_full[later, :] * unit, axis=1, keepdims=True)
                    vecs[later, :] = vecs[later, :] - coef * unit
            basis[block, :] = jnp.concatenate(done, axis=0)

        high, low = halves(basis[...])
        b_split[0:rank] = high
        b_split[rank:2 * rank] = low

        groups = ff // cw

        @pl.loop(0, groups)
        def _(i):
            group = lax.rem(own_group + 1 + i, groups)
            cols = pl.ds(pl.multiple_of(group * cw, cw), cw)
            both = jnp.dot(b_split[...], m_hi[:, cols], preferred_element_type=F32)
            both += jnp.dot(b_split[...], m_lo[:, cols], preferred_element_type=F32)
            q_part[:, cols] = both[0:rank] + both[rank:2 * rank]

            for j in range(members):
                target = (group * members + j) * q_cuts[2]

                @pl.when(target != me)
                def _():
                    pltpu.make_async_remote_copy(
                        src_ref=q_part.at[piece(q_cuts, q_part.shape, target)],
                        dst_ref=q_recv.at[lax.rem(target - me + count, count) - 1],
                        send_sem=q_rs_send, recv_sem=q_rs_recv,
                        device_id=(target,), device_id_type=MESH,
                    ).start()

        add_up(
            q_cuts, q_part, q_full, q_recv, q_rs_recv, q_ag_send, q_ag_recv.at[own_group], count
        )

        @pl.when(step < ITERS - 1)
        def _():
            @pl.loop(0, step_cols)
            def _(i):
                group = lax.rem(own_group - i + step_cols, step_cols)
                await_group(group)
                absorb(q_full, columns(group))

            drain_sends(q_cuts, q_recv, q_rs_send, q_ag_send)
            settle()

    tall = basis[...].T
    high, low = halves(tall)
    b_tall[:, 0:rank] = high
    b_tall[:, rank:2 * rank] = high
    b_tall[:, 2 * rank:3 * rank] = low

    @pl.loop(0, step_cols)
    def _(i):
        group = lax.rem(own_group - i + step_cols, step_cols)
        await_group(group)
        cols = columns(group)
        high, low = halves(q_full[:, cols])
        factor = jnp.concatenate([high, low, high], axis=0)
        q_split[:, cols] = factor
        recon = jnp.dot(b_tall[...], factor, preferred_element_type=F32)
        merged = m_hi[:, cols].astype(F32) + m_lo[:, cols].astype(F32)
        err_v[:, cols] = (merged - recon).astype(BF16)

    drain_sends(q_cuts, q_recv, q_rs_send, q_ag_send)
    q_out[...] = q_full[...]

    own = master_ref.shape[1]
    if own % 128 == 0:
        mine = q_split[:, pl.ds(pl.multiple_of(me * own, own), own)]
    else:
        base = pl.multiple_of((me * own) // 128 * 128, 128)
        block = q_split[:, pl.ds(base, 128)].astype(F32)
        shift = lax.rem(128 - lax.rem(me * own, 128), 128)
        mine = pltpu.roll(block, shift, 1)[:, 0:own].astype(BF16)
    master_out[...] = master_ref[...] - 0.5 * jnp.dot(b_tall[...], mine, preferred_element_type=F32)


def shards(inputs, out_grads, error_in, q_start, master):
    count = lax.axis_size(AXIS)
    tokens, width = inputs.shape
    ff = out_grads.shape[1]
    rank = q_start.shape[0]
    steps = ff // 512
    hbm_spec = pl.BlockSpec(memory_space=pltpu.HBM)
    vmem_spec = pl.BlockSpec(memory_space=pltpu.VMEM)
    p_cuts, q_cuts = split_tiles(count, rank, width), split_tiles(count, rank, ff)
    dma = pltpu.SemaphoreType.DMA
    return pl.pallas_call(
        functools.partial(kernel, count),
        out_shape=(
            pltpu.VMEM(error_in.shape, BF16),
            pltpu.VMEM(q_start.shape, F32),
            pltpu.VMEM(master.shape, F32),
        ),
        in_specs=[hbm_spec] * 3 + [vmem_spec] * 2,
        out_specs=(vmem_spec, vmem_spec, vmem_spec),
        scratch_shapes=[
            pltpu.VMEM((tokens, width), BF16),
            pltpu.VMEM((width, tokens), BF16),
            pltpu.VMEM((tokens, ff), BF16),
            pltpu.VMEM((width, ff), BF16),
            pltpu.VMEM((width, ff), BF16),
            pltpu.VMEM((rank, ff), F32),
            pltpu.VMEM((rank, ff), F32),
            pltpu.VMEM((count - 1, rank // q_cuts[0], ff // q_cuts[1]), F32),
            pltpu.VMEM((3 * rank, ff), BF16),
            pltpu.VMEM((rank, width), F32),
            pltpu.VMEM((rank, width), F32),
            pltpu.VMEM((count - 1, rank // p_cuts[0], width // p_cuts[1]), F32),
            pltpu.VMEM((rank, width), F32),
            pltpu.VMEM((rank, width), F32),
            pltpu.VMEM((2 * rank, width), BF16),
            pltpu.VMEM((width, 3 * rank), BF16),
            pltpu.VMEM((width, 2 * rank), F32),
            dma, dma((steps,)), dma((steps,)),
            dma, dma, dma, dma, dma, dma, dma, dma((steps,)),
        ],
        compiler_params=pltpu.CompilerParams(
            collective_id=0, has_side_effects=True, vmem_limit_bytes=44 * 1024 * 1024
        ),
    )(inputs, out_grads, error_in, q_start, master)


def solution(mesh):
    return jax.shard_map(
        shards,
        mesh=mesh,
        in_specs=(P("rep", None), P("rep", None), P("rep", None, None), P(), P(None, "rep")),
        out_specs=(P("rep", None, None), P(), P(None, "rep")),
        check_vma=False,
    )
```

time: 1180 us -> 162 us (0.14); the launches traced: 1160 us -> 162 us
  waiting for transfers between devices: 755 us -> 0 us
  matrix products: 229 us -> 0 us
  Pallas kernels: 0 us -> 155 us
  between operations: 83.2 us -> 0.65 us
  other arithmetic: 69.8 us -> 0 us
  local copies, waits for them, and re-layouts: 25.2 us -> 6.02 us
    psum x6 -> x0, waiting for transfers between devices: 754 us -> none  [the longest x3 384 us: shards(): factor = lax.psum(local_q, 'rep') / count]
    dot_general x200 -> x0, matrix products: 229 us -> none  [the longest x96 89.7 us: orthonormal(): coef = jnp.dot(basis, vector, precision=lax.Precision.HIGHEST)]
    pallas_call x0 -> x1, Pallas kernels: none -> 155 us  [shards(): pl.pallas_call(functools.partial(kernel, count), out_shape=(pltpu.VMEM(er...]
    reduce_sum x96 -> x0, other arithmetic: 57.8 us -> none  [orthonormal(): basis = basis.at[k].set(vector / jnp.sqrt(jnp.sum(vector * vector) + 1.0))]
  transfers between devices with their start and end apart: 6 -> 0, of which waited for: 6 -> 0; matrix products, arithmetic and copies ran while one was open for 0% -> 0% of each run, Pallas kernels for 0% -> 0%
where the time goes in v1:
time: 162 us
  Pallas kernels  155 us (96%)
  local copies, waits for them, and re-layouts  6.02 us (4%)
    pallas_call x1, Pallas kernels, shards(): pl.pallas_call(functools.partial(kernel, count), out_shape=(pltpu.VMEM(er...  155 us
    unnamed x5, local copies, waits for them, and re-layouts  6.02 us

profile of v1, /device:TPU:27, one launch (start us, length us, event | category | flops | bytes accessed | tf_op | source)
XLA Modules:
  0.0 161.8 jit_solution(3413040326139709061)
XLA Ops:
  0.6 0.0 copy-start
  0.6 1.0 copy-done
  1.7 155.1 %shard_map.76 = (bf16[1,1024,4096]{2,1,0:T(8,128)(2,1)S(1)}, f32[32,4096]{1,0:T(8,128)S(1)}, f32[1024,128]{1,0:T(8,128)S(1)}) custom-call(bf16[512,1024]{1,0:T(8,128)(2,1)} %x_hbm.1, bf16[512,4096]{1,0:T(8,128)(2,1)} %dy_hbm.1, bf16[1,1024,4096]{2,1,0:T(8,128)(2,1)} %err_hbm.1, f32[32,4096]{1,0:T(8,128)S(1)} %copy-done, f32[1024,128]{1,0:T(8,128)} %master_ref.1), custom_call_target="tpu_custom_call" | custom-call | tf_op jit(solution)/shard_map/pallas_call | solution.py:293
  156.8 3.4 %copy.11 = bf16[1,1024,4096]{2,1,0:T(8,128)(2,1)} copy(bf16[1,1024,4096]{2,1,0:T(8,128)(2,1)S(1)} %get-tuple-element.3) | data formatting | bytes 16777216
  160.2 0.8 copy.12
  161.0 0.8 copy.13
Async XLA Ops:
  0.6 1.0 copy-start

commit v2 on v1

--- a/solution.py
+++ b/solution.py
@@ -68,15 +68,9 @@
         else:
             pl.when(is_owner(cuts, device))(body)
 
-    def send_piece(cuts, part, recv, send_sem, recv_sem, target):
-        def body():
-            pltpu.make_async_remote_copy(
-                src_ref=part.at[piece(cuts, part.shape, target)],
-                dst_ref=recv.at[lax.rem(target - me + count, count) - 1],
-                send_sem=send_sem, recv_sem=recv_sem,
-                device_id=(target,), device_id_type=MESH,
-            ).start()
-        guarded(cuts, target, body)
+    def after(d):
+        device = me + d
+        return jnp.where(device < count, device, device - count)
 
     def drain(recv, sem, pieces):
         if pieces:
@@ -102,7 +96,7 @@
                 pltpu.make_async_remote_copy(
                     src_ref=full.at[mine], dst_ref=full.at[mine],
                     send_sem=ag_send, recv_sem=ag_recv,
-                    device_id=(lax.rem(me + d, count),), device_id_type=MESH,
+                    device_id=(after(d),), device_id_type=MESH,
                 ).start()
 
         either(cuts, body, lambda: None)
@@ -152,6 +146,21 @@
     def settle():
         flat = p_tall[...].T
         p_part[...] = flat[0:rank] + flat[rank:2 * rank]
+
+        @pl.loop(1, count)
+        def _(d):
+            target = after(d)
+
+            def send():
+                pltpu.make_async_remote_copy(
+                    src_ref=p_part.at[piece(p_cuts, p_part.shape, target)],
+                    dst_ref=p_recv.at[d - 1],
+                    send_sem=p_rs_send, recv_sem=p_rs_recv,
+                    device_id=(target,), device_id_type=MESH,
+                ).start()
+
+            guarded(p_cuts, target, send)
+
         p_tall[...] = jnp.zeros_like(p_tall)
 
     pltpu.make_async_copy(x_hbm, x_v, load_sem).wait()
@@ -169,15 +178,11 @@
         m_lo[:, cols] = low
         absorb(start_ref, cols)
 
+    pl.semaphore_wait(barrier, count - 1)
     settle()
-    pl.semaphore_wait(barrier, count - 1)
 
     @pl.loop(0, ITERS)
     def _(step):
-        @pl.loop(1, count)
-        def _(d):
-            send_piece(p_cuts, p_part, p_recv, p_rs_send, p_rs_recv, lax.rem(me + d, count))
-
         add_up(p_cuts, p_part, p_full, p_recv, p_rs_recv, p_ag_send, p_ag_recv, 1)
         p_owners = p_cuts[0] * p_cuts[1]
         either(
@@ -185,7 +190,6 @@
             lambda: drain(p_recv, p_ag_recv, p_owners - 1),
             lambda: drain(p_recv, p_ag_recv, p_owners),
         )
-        drain_sends(p_cuts, p_recv, p_rs_send, p_ag_send)
 
         vecs[...] = p_full[...]
         for base in range(0, rank, 8):
@@ -237,6 +241,8 @@
             q_cuts, q_part, q_full, q_recv, q_rs_recv, q_ag_send, q_ag_recv.at[own_group], count
         )
 
+        drain_sends(p_cuts, p_recv, p_rs_send, p_ag_send)
+
         @pl.when(step < ITERS - 1)
         def _():
             @pl.loop(0, step_cols)
@@ -245,8 +251,8 @@
                 await_group(group)
                 absorb(q_full, columns(group))
 
+            settle()
             drain_sends(q_cuts, q_recv, q_rs_send, q_ag_send)
-            settle()
 
     tall = basis[...].T
     high, low = halves(tall)

time: 162 us -> 162 us (level)
  no operation moved by 1% of the time
where the time goes in v2:
time: 162 us
  Pallas kernels  155 us (96%)
  local copies, waits for them, and re-layouts  6.02 us (4%)
    pallas_call x1, Pallas kernels, shards(): pl.pallas_call(functools.partial(kernel, count), out_shape=(pltpu.VMEM(er...  155 us
    unnamed x5, local copies, waits for them, and re-layouts  6.02 us

profile of v2, /device:TPU:27, one launch (start us, length us, event | category | flops | bytes accessed | tf_op | source)
XLA Modules:
  0.0 161.7 jit_solution(9686584422494774823)
XLA Ops:
  0.6 0.0 copy-start
  0.6 1.0 copy-done
  1.7 155.0 %shard_map.76 = (bf16[1,1024,4096]{2,1,0:T(8,128)(2,1)S(1)}, f32[32,4096]{1,0:T(8,128)S(1)}, f32[1024,128]{1,0:T(8,128)S(1)}) custom-call(bf16[512,1024]{1,0:T(8,128)(2,1)} %x_hbm.1, bf16[512,4096]{1,0:T(8,128)(2,1)} %dy_hbm.1, bf16[1,1024,4096]{2,1,0:T(8,128)(2,1)} %err_hbm.1, f32[32,4096]{1,0:T(8,128)S(1)} %copy-done, f32[1024,128]{1,0:T(8,128)} %master_ref.1), custom_call_target="tpu_custom_call" | custom-call | tf_op jit(solution)/shard_map/pallas_call | solution.py:299
  156.7 3.4 %copy.11 = bf16[1,1024,4096]{2,1,0:T(8,128)(2,1)} copy(bf16[1,1024,4096]{2,1,0:T(8,128)(2,1)S(1)} %get-tuple-element.3) | data formatting | bytes 16777216
  160.1 0.8 copy.12
  160.9 0.8 copy.13
Async XLA Ops:
  0.6 1.0 copy-start
